TPU v7x, 256 devices: a whole 4x4x8 slice. The times are simulated.
256 devices in a mesh: beam: 32 (over y, z), mp: 8 (over x, core).
Axes of the slice: x: 4, y: 4, z: 8, core: 2. Of those that a mesh axis runs over, the one named last changes fastest.
Arguments:
- queries: bfloat16 [512, 8192], P('beam', 'mp'), may hold values from -100 to 100
- fresh_keys: bfloat16 [512, 1024], P('beam', 'mp'), may hold values from -5 to 5
- fresh_values: bfloat16 [512, 1024], P('beam', 'mp'), may hold values from -5 to 5
- key_pool: bfloat16 [2048, 8, 128, 128], P('beam', 'mp'), may hold values from -5 to 5
- value_pool: bfloat16 [2048, 8, 128, 128], P('beam', 'mp'), may hold values from -5 to 5
- page_table: int32 [512, 4], P('beam'), may hold values from 0 to 63, as said below
- lengths: int32 [512], replicated, may hold values from 2 to 511, as said below
- score_weight: bfloat16 [8192], P('mp'), may hold values from -0.0625 to 0.0625
- running_min: float32 [512], P('beam'), may hold values from 0.2 to 0.9
- boundary: int32 [512], P('beam'), may hold values 0 or 1
- parents: int32 [512], replicated, may hold values from 0 to 511, as said below
- homes: int32 [512], replicated, may hold values from 0 to 511, as said below
Outputs:
- attention: bfloat16 [512, 8192], P('beam', 'mp')
- step_score: float32 [512], P('beam')
- child_score: float32 [512], P('beam')
- new_keys: bfloat16 [2048, 8, 128, 128], P('beam', 'mp')
- new_values: bfloat16 [2048, 8, 128, 128], P('beam', 'mp')
Inputs may be any that keep to these rules, and one draw needn't show every extreme that they name: `page_table`: the rows of the 16 old beams of one device together name each of that device's 16 * 4 slots once. `lengths`: some old beam that has a new beam descending from it has the largest length. Of the new beams stored on one device of the beam axis (positions homes[c] // 16 equal), at most one of them has its parent on any one device (parents[c] // 16 equal); in every draw some pairs of devices have exactly 1. homes is a permutation of the positions 0 to 511.
All inputs are finite; a program needn't handle non-finite values. No bound on the sum of `boundary` on one device may be relied on, other than what follows from the above.
Results may differ from a plain program's by a relative error of at most 0.0049.
Values may be sent and summed in bfloat16 or wider, within the bound.
A program may use at most 64 MiB of HBM per device.

v0:
```python
import math

import jax
import jax.numpy as jnp
from jax import lax
from jax.sharding import PartitionSpec as P


def sent_to_all(array, axis):
    copies = jnp.broadcast_to(array, (lax.axis_size(axis), *array.shape))
    return lax.all_to_all(copies, axis, split_axis=0, concat_axis=0, tiled=True)


def over_copies(array, axis):
    return sent_to_all(array, axis).sum(axis=0)


def packed_total(arrays, axis):
    ends = [0]
    for a in arrays:
        ends.append(ends[-1] + a.size)
    running = over_copies(jnp.concatenate([a.ravel() for a in arrays]), axis)
    return tuple((running[b:e].reshape(a.shape) for a, b, e in zip(arrays, ends, ends[1:])))


def laid_out(parts, dim):
    parts = jnp.moveaxis(parts, 0, dim)
    dims = parts.shape
    return parts.reshape(*dims[:dim], dims[dim] * dims[dim + 1], *dims[dim + 2 :])


def collect(array, axis, dim):
    return laid_out(sent_to_all(array, axis), dim)


def per_device(
    queries,
    fresh_keys,
    fresh_values,
    key_pool,
    value_pool,
    page_table,
    lengths,
    score_weight,
    running_min,
    boundary,
    parents,
    homes,
):
    ranks = lax.axis_size("beam")
    rank = lax.axis_index("beam")
    local_beams, pages = page_table.shape
    kv_local = key_pool.shape[1]
    page_length = key_pool.shape[2]
    head_dim = key_pool.shape[3]
    heads_local = queries.shape[1] // head_dim
    group = heads_local // kv_local
    beams = lengths.shape[0]
    capacity = (local_beams + ranks - 1) // ranks
    slot_cap = capacity * pages
    buffer_rows = ranks * slot_cap
    everyone = jnp.arange(beams, dtype=jnp.int32)
    page_ids = jnp.arange(pages, dtype=jnp.int32)
    token_grid = page_ids[:, None] * page_length + jnp.arange(page_length, dtype=jnp.int32)[None, :]
    parent_hit = parents[:, None] == everyone[None, :]
    parent_len = jnp.sum(jnp.where(parent_hit, lengths[None, :], 0), axis=1)
    used_pages = parent_len // page_length + 1
    source = parents // local_beams
    destination = homes // local_beams
    earlier = everyone[None, :] < everyone[:, None]
    same_pair = (
        (source[:, None] == source[None, :])
        & (destination[:, None] == destination[None, :])
        & earlier
    )
    offset_table = jnp.sum(jnp.where(same_pair, used_pages[None, :], 0), axis=1)
    sending = (source == rank)[:, None] & (page_ids[None, :] < used_pages[:, None])
    dest_rows = destination[:, None] * slot_cap + offset_table[:, None] + page_ids[None, :]
    dest_rows = jnp.where(sending, dest_rows, buffer_rows)
    local_parent = jnp.clip(parents - rank * local_beams, 0, local_beams - 1)
    source_slots = page_table[local_parent]
    send_table = (
        jnp.zeros((buffer_rows,), jnp.int32)
        .at[dest_rows.reshape(-1)]
        .set(source_slots.reshape(-1), mode="drop")
    )
    positions = rank * local_beams + jnp.arange(local_beams, dtype=jnp.int32)
    child_hit = homes[None, :] == positions[:, None]
    child_source = jnp.sum(jnp.where(child_hit, source[None, :], 0), axis=1)
    child_offset = jnp.sum(jnp.where(child_hit, offset_table[None, :], 0), axis=1)
    child_len = jnp.sum(jnp.where(child_hit, parent_len[None, :], 0), axis=1)
    child_parent = jnp.sum(jnp.where(child_hit, parents[None, :], 0), axis=1)
    recv_rows = jnp.clip(
        child_source[:, None] * slot_cap + child_offset[:, None] + page_ids[None, :],
        0,
        buffer_rows - 1,
    )
    own_len = lax.dynamic_slice_in_dim(lengths, rank * local_beams, local_beams)
    last_page = jnp.take_along_axis(page_table, (own_len // page_length)[:, None], axis=1)[:, 0]
    offset_in = own_len % page_length
    keys_now = key_pool.at[last_page, :, offset_in, :].set(
        fresh_keys.reshape(local_beams, kv_local, head_dim)
    )
    values_now = value_pool.at[last_page, :, offset_in, :].set(
        fresh_values.reshape(local_beams, kv_local, head_dim)
    )
    scale = 1.0 / math.sqrt(head_dim)
    key_rows = keys_now[page_table]
    value_rows = values_now[page_table]
    query = queries.reshape(local_beams, kv_local, group, head_dim)
    scores = (
        jnp.einsum("bhgd,bphtd->bhgpt", query, key_rows, preferred_element_type=jnp.float32) * scale
    )
    live_own = (token_grid[None] <= own_len[:, None, None])[:, None, None]
    scores = jnp.where(live_own, scores, -jnp.inf)
    flattened_scores = scores.reshape(local_beams, kv_local, group, pages * page_length)
    weights = jax.nn.softmax(flattened_scores, axis=-1).astype(jnp.bfloat16).reshape(scores.shape)
    mixed = jnp.einsum("bhgpt,bphtd->bhgd", weights, value_rows, preferred_element_type=jnp.float32)
    attention = mixed.reshape(local_beams, heads_local * head_dim).astype(jnp.bfloat16)
    as_float = attention.astype(jnp.float32)
    partial_square = jnp.sum(as_float * as_float, axis=1)
    partial_dot = jnp.sum(as_float * score_weight.astype(jnp.float32)[None, :], axis=1)
    total_square, total_dot = packed_total((partial_square, partial_dot), "mp")
    width = heads_local * head_dim * lax.axis_size("mp")
    step_score = jax.nn.sigmoid(total_dot * lax.rsqrt(total_square / width + 1e-06))
    updated = jnp.where(boundary == 1, jnp.minimum(running_min, step_score), running_min)
    every_updated = collect(updated, "beam", 0)
    child_score = jnp.sum(
        jnp.where(child_parent[:, None] == everyone[None, :], every_updated[None, :], 0.0), axis=1
    )
    moved_keys, moved_values = (
        lax.all_to_all(keys_now[send_table], "beam", split_axis=0, concat_axis=0, tiled=True),
        lax.all_to_all(values_now[send_table], "beam", split_axis=0, concat_axis=0, tiled=True),
    )
    landed_keys = moved_keys[recv_rows]
    landed_values = moved_values[recv_rows]
    live_child = (token_grid[None] <= child_len[:, None, None])[:, :, None, :, None]
    zero = jnp.zeros((), landed_keys.dtype)
    new_keys = jnp.where(live_child, landed_keys, zero).reshape(
        local_beams * pages, kv_local, page_length, head_dim
    )
    new_values = jnp.where(live_child, landed_values, zero).reshape(
        local_beams * pages, kv_local, page_length, head_dim
    )
    return (attention, step_score, child_score, new_keys, new_values)


def solution(mesh):
    in_specs = (
        P("beam", "mp"),
        P("beam", "mp"),
        P("beam", "mp"),
        P("beam", "mp", None, None),
        P("beam", "mp", None, None),
        P("beam", None),
        P(),
        P("mp"),
        P("beam"),
        P("beam"),
        P(),
        P(),
    )
    out_specs = (
        P("beam", "mp"),
        P("beam"),
        P("beam"),
        P("beam", "mp", None, None),
        P("beam", "mp", None, None),
    )
    return jax.shard_map(
        per_device, mesh=mesh, in_specs=in_specs, out_specs=out_specs, check_vma=False
    )
```

profile of v0, /device:TPU:1, one launch (start us, length us, event | category | flops | bytes accessed | tf_op | source)
XLA Modules:
  0.0 265.8 jit_solution(2704530823482767814)
XLA Ops:
  0.6 3.2 %copy.52 = bf16[64,1,128,128]{3,2,1,0:T(8,128)(2,1)} copy(bf16[64,1,128,128]{3,2,1,0:T(8,128)(2,1)} %param.15) | data formatting | bytes 4194304
  3.8 0.6 copy-done.8
  4.6 0.7 gather_fusion.7
  5.7 2.3 scatter_fusion
  8.0 3.9 %gather_fusion = bf16[64,128,128]{2,1,0:T(8,128)(2,1)} fusion(bf16[64,128,128]{2,1,0:T(8,128)(2,1)} %scatter_fusion, s32[1024]{0:T(1024)S(1)} %pad_clamp_fusion.3), kind=kCustom, calls=%fused_computation | custom fusion | bytes 4194560 | tf_op jit(solution)/shard_map/gather | solution.py:108
  11.9 1.3 scatter_fusion.1
  13.2 2.1 gather_fusion.1
  15.4 2.5 fusion.30
  19.3 6.4 %all-to-all-start = ((f32[8,1,32]{2,1,0:T(1,128)}), f32[8,1,32]{2,1,0:T(1,128)S(1)}, u32[]{:S(2)}, u32[]{:S(2)}) async-start(f32[8,1,32]{2,1,0:T(1,128)} %broadcast_in_dim.168), calls=%async_computation | async-start | bytes 8192 | tf_op jit(solution)/shard_map/all_to_all | solution.py:11
  26.5 1.0 gather_fusion.2
  28.2 8.0 %scatter_custom_fusion.2 = s32[128]{0:T(128)S(1)} fusion(s32[2048]{0:T(1024)S(1)} %bitcast.87, s32[2048]{0:T(1024)S(1)} %reshape.443, s32[]{:T(128)} %constant.97.clone.1), kind=kCustom, calls=%fused_computation.110 | custom fusion | bytes 516 | tf_op jit(solution)/shard_map/scatter | solution.py:85
  37.5 10.6 %all-to-all-start.1 = ((f32[32,1,16]{2,1,0:T(1,128)}), f32[32,1,16]{2,1,0:T(1,128)S(1)}, u32[]{:S(2)}, u32[]{:S(2)}) async-start(f32[32,1,16]{2,1,0:T(1,128)} %broadcast_in_dim.171), calls=%async_computation.1 | async-start | bytes 32768 | tf_op jit(solution)/shard_map/all_to_all | solution.py:11
  48.1 4.7 %gather_fusion.3 = bf16[128,128,128]{2,1,0:T(8,128)(2,1)} fusion(bf16[64,128,128]{2,1,0:T(8,128)(2,1)} %scatter_fusion, s32[1024]{0:T(1024)S(1)} %pad_clamp_fusion.1), kind=kCustom, calls=%fused_computation.3 | custom fusion | bytes 8389120 | tf_op jit(solution)/shard_map/gather | solution.py:132
  52.7 3.9 %all-to-all-done.1 = f32[32,1,16]{2,1,0:T(1,128)S(1)} async-done(((f32[32,1,16]{2,1,0:T(1,128)}), f32[32,1,16]{2,1,0:T(1,128)S(1)}, u32[]{:S(2)}, u32[]{:S(2)}) %all-to-all-start.1) | async-done | bytes 2080 | tf_op jit(solution)/shard_map/all_to_all | solution.py:11
  56.7 5.4 %all-to-all-start.2 = ((bf16[128,1,128,128]{3,2,1,0:T(8,128)(2,1)}), bf16[128,1,128,128]{3,2,1,0:T(8,128)(2,1)}, u32[]{:S(2)}, u32[]{:S(2)}) async-start(bf16[128,1,128,128]{3,2,1,0:T(8,128)(2,1)} %bitcast.78), calls=%async_computation.2 | async-start | bytes 8388608 | tf_op jit(solution)/shard_map/all_to_all | solution.py:132
  62.1 3.1 %gather_fusion.5 = bf16[128,128,128]{2,1,0:T(8,128)(2,1)} fusion(bf16[64,128,128]{2,1,0:T(8,128)(2,1)S(1)} %scatter_fusion.1, s32[1024]{0:T(1024)S(1)} %pad_clamp_fusion.1), kind=kCustom, calls=%fused_computation.5 | custom fusion | bytes 8389120 | tf_op jit(solution)/shard_map/gather | solution.py:133
  65.1 89.5 %all-to-all-done.2 = bf16[128,1,128,128]{3,2,1,0:T(8,128)(2,1)} async-done(((bf16[128,1,128,128]{3,2,1,0:T(8,128)(2,1)}), bf16[128,1,128,128]{3,2,1,0:T(8,128)(2,1)}, u32[]{:S(2)}, u32[]{:S(2)}) %all-to-all-start.2) | async-done | bytes 4194336 | tf_op jit(solution)/shard_map/all_to_all | solution.py:132
  154.7 9.4 %all-to-all-start.3 = ((bf16[128,1,128,128]{3,2,1,0:T(8,128)(2,1)}), bf16[128,1,128,128]{3,2,1,0:T(8,128)(2,1)}, u32[]{:S(2)}, u32[]{:S(2)}) async-start(bf16[128,1,128,128]{3,2,1,0:T(8,128)(2,1)} %bitcast.77), calls=%async_computation.3 | async-start | bytes 8388608 | tf_op jit(solution)/shard_map/all_to_all | solution.py:133
  165.9 0.7 reduce.13
  166.7 0.7 select_reduce_fusion.2
  167.4 3.1 %gather_fusion.4 = bf16[64,128,128]{2,1,0:T(8,128)(2,1)S(1)} fusion(bf16[128,128,128]{2,1,0:T(8,128)(2,1)} %bitcast.20, s32[1024]{0:T(1024)S(1)} %pad_clamp_fusion), kind=kCustom, calls=%fused_computation.4 | custom fusion | bytes 4194560 | tf_op jit(solution)/shard_map/gather | solution.py:135
  170.5 86.2 %all-to-all-done.3 = bf16[128,1,128,128]{3,2,1,0:T(8,128)(2,1)} async-done(((bf16[128,1,128,128]{3,2,1,0:T(8,128)(2,1)}), bf16[128,1,128,128]{3,2,1,0:T(8,128)(2,1)}, u32[]{:S(2)}, u32[]{:S(2)}) %all-to-all-start.3) | async-done | bytes 4194336 | tf_op jit(solution)/shard_map/all_to_all | solution.py:133
  256.8 4.3 %gather_fusion.6 = bf16[64,128,128]{2,1,0:T(8,128)(2,1)} fusion(bf16[128,128,128]{2,1,0:T(8,128)(2,1)} %bitcast.25, s32[1024]{0:T(1024)S(1)} %pad_clamp_fusion), kind=kCustom, calls=%fused_computation.6 | custom fusion | bytes 4194560 | tf_op jit(solution)/shard_map/gather | solution.py:136
  261.1 4.7 %fusion = (bf16[64,1,128,128]{3,2,1,0:T(8,128)(2,1)}, bf16[64,1,128,128]{3,2,1,0:T(8,128)(2,1)}) fusion(bf16[64,128,128]{2,1,0:T(8,128)(2,1)} %gather_fusion.6, pred[64,128]{1,0:T(8,128)(4,1)S(1)} %broadcast_compare_fusion, bf16[64,128,128]{2,1,0:T(8,128)(2,1)S(1)} %gather_fusion.4), kind=kLoop, calls=%fused_computation.12 | loop fusion | flops 2097152 | bytes 8396800
  (72 shorter events, 6.4 us)
Async XLA Ops:
  3.8 0.7 copy-start.8
  3.8 0.8 copy-start
  3.8 1.6 copy-start.9
  3.8 1.9 copy-start.4
  3.8 1.9 copy-start.6
  8.0 3.9 %copy-start.1 = (bf16[64,1,128,128]{3,2,1,0:T(8,128)(2,1)S(1)}, bf16[64,1,128,128]{3,2,1,0:T(8,128)(2,1)}, u32[]{:S(2)}) copy-start(bf16[64,1,128,128]{3,2,1,0:T(8,128)(2,1)} %param.16) | copy-start | bytes 6291460
  8.0 3.9 %copy-start.7 = (bf16[16,128]{1,0:T(8,128)(2,1)S(1)}, bf16[16,128]{1,0:T(8,128)(2,1)}, u32[]{:S(2)}) copy-start(bf16[16,128]{1,0:T(8,128)(2,1)} %param.14) | copy-start | bytes 12292
  15.4 2.7 %copy-start.2 = (bf16[64,128,128]{2,1,0:T(8,128)(2,1)S(1)}, bf16[64,128,128]{2,1,0:T(8,128)(2,1)}, u32[]{:S(2)}) copy-start(bf16[64,128,128]{2,1,0:T(8,128)(2,1)} %gather_fusion.1) | copy-start | bytes 6291460
  15.4 10.3 %copy-start.3 = (s32[512]{0:T(512)S(1)}, s32[512]{0:T(512)}, u32[]{:S(2)}) copy-start(s32[512]{0:T(512)} %param.22) | copy-start | bytes 6148
  15.4 10.7 %copy-start.5 = (s32[512]{0:T(512)S(1)}, s32[512]{0:T(512)}, u32[]{:S(2)}) copy-start(s32[512]{0:T(512)} %param.23) | copy-start | bytes 6148
  18.6 17.6 %copy-start.10 = (f32[16]{0:T(128)S(1)}, f32[16]{0:T(128)}, u32[]{:S(2)}) copy-start(f32[16]{0:T(128)} %param.20) | copy-start | bytes 196
  18.6 17.6 %copy-start.11 = (s32[16]{0:T(128)S(1)}, s32[16]{0:T(128)}, u32[]{:S(2)}) copy-start(s32[16]{0:T(128)} %param.21) | copy-start | bytes 196
  19.3 16.9 %all-to-all-start = ((f32[8,1,32]{2,1,0:T(1,128)}), f32[8,1,32]{2,1,0:T(1,128)S(1)}, u32[]{:S(2)}, u32[]{:S(2)}) async-start(f32[8,1,32]{2,1,0:T(1,128)} %broadcast_in_dim.168), calls=%async_computation | async-start | bytes 8192 | tf_op jit(solution)/shard_map/all_to_all | solution.py:11
  37.5 19.2 %all-to-all-start.1 = ((f32[32,1,16]{2,1,0:T(1,128)}), f32[32,1,16]{2,1,0:T(1,128)S(1)}, u32[]{:S(2)}, u32[]{:S(2)}) async-start(f32[32,1,16]{2,1,0:T(1,128)} %broadcast_in_dim.171), calls=%async_computation.1 | async-start | bytes 32768 | tf_op jit(solution)/shard_map/all_to_all | solution.py:11
  56.7 98.0 %all-to-all-start.2 = ((bf16[128,1,128,128]{3,2,1,0:T(8,128)(2,1)}), bf16[128,1,128,128]{3,2,1,0:T(8,128)(2,1)}, u32[]{:S(2)}, u32[]{:S(2)}) async-start(bf16[128,1,128,128]{3,2,1,0:T(8,128)(2,1)} %bitcast.78), calls=%async_computation.2 | async-start | bytes 8388608 | tf_op jit(solution)/shard_map/all_to_all | solution.py:132
  154.7 102.1 %all-to-all-start.3 = ((bf16[128,1,128,128]{3,2,1,0:T(8,128)(2,1)}), bf16[128,1,128,128]{3,2,1,0:T(8,128)(2,1)}, u32[]{:S(2)}, u32[]{:S(2)}) async-start(bf16[128,1,128,128]{3,2,1,0:T(8,128)(2,1)} %bitcast.77), calls=%async_computation.3 | async-start | bytes 8388608 | tf_op jit(solution)/shard_map/all_to_all | solution.py:133
where the time goes:
time: 271 us; the launch traced here: 266 us
  waiting for transfers between devices  180 us (66%)
  local copies, waits for them, and re-layouts  41.7 us (15%)
  starting transfers between devices  31.8 us (12%)
  other arithmetic  8.64 us (3%)
  matrix products  3 us (1%)
    all_to_all x1, waiting for transfers between devices, per_device(): lax.all_to_all(keys_now[send_table], 'beam', split_axis=0, concat_axis=0,...  89.5 us
    all_to_all x1, waiting for transfers between devices, per_device(): lax.all_to_all(values_now[send_table], 'beam', split_axis=0, concat_axis=...  86.2 us
    all_to_all x2, starting transfers between devices, sent_to_all(): return lax.all_to_all(copies, axis, split_axis=0, concat_axis=0, tiled=True)  17 us
    all_to_all x1, starting transfers between devices, per_device(): lax.all_to_all(values_now[send_table], 'beam', split_axis=0, concat_axis=...  9.41 us
    scatter x1, local copies, waits for them, and re-layouts, per_device(): send_table = jnp.zeros((buffer_rows,), jnp.int32).at[dest_rows.reshape(-1...  8.04 us
    all_to_all x1, starting transfers between devices, per_device(): lax.all_to_all(keys_now[send_table], 'beam', split_axis=0, concat_axis=0,...  5.43 us
  transfers between devices with their start and end apart: 4, of which 3 were waited for; matrix products, arithmetic and copies ran while one was open for 9% of the time, Pallas kernels for 0%

commit v1 on v0

--- a/solution.py
+++ b/solution.py
@@ -1,9 +1,335 @@
+import functools
 import math
 
 import jax
 import jax.numpy as jnp
 from jax import lax
+from jax.experimental import pallas as pl
+from jax.experimental.pallas import tpu as pltpu
 from jax.sharding import PartitionSpec as P
+
+WAIT = 4
+Z_SLOTS = 80
+Y_SLOTS = 44
+Z_BUFS = 8
+Y_BUFS = 4
+Y_WAIT = 3
+RING_Z = 8
+RING_Y = 4
+
+
+def pick(mask, values, axis):
+    return jnp.sum(jnp.where(mask, values, 0), axis=axis)
+
+
+def plan(parents, homes, lengths, page_table, fresh_at, rank):
+    beams = parents.shape[0]
+    local, pages = page_table.shape
+    pool = local * pages
+    every = jnp.arange(beams, dtype=jnp.int32)
+    q = pick(homes[None, :] == every[:, None], parents[None, :], 1)
+    up = pick(q[:, None] == every[None, :], lengths[None, :], 1) // 128 + 1
+    src, dst = q // local, every // local
+    sy, sz, dy, dz = src // RING_Z, src % RING_Z, dst // RING_Z, dst % RING_Z
+    d = (dz - sz) % RING_Z
+    sib = q[:, None] == q[None, :]
+    far_p = jnp.max(jnp.where(sib & (d < 4)[None, :], d[None, :], 0), axis=1)
+    far_m = jnp.max(jnp.where(sib & (d > 4)[None, :], RING_Z - d[None, :], 0), axis=1)
+    far_4 = jnp.max(jnp.where(sib & (d == 4)[None, :], 1, 0), axis=1) > 0
+    plus4 = far_4 & ((far_p > far_m) | ((far_p == far_m) & (q % 2 == 1)))
+    a = jnp.where(plus4, 4, far_p)
+    b = jnp.where(far_4 & ~plus4, 4, far_m)
+    first = jnp.max(jnp.where(sib & (every[None, :] < every[:, None]), 1, 0), axis=1) == 0
+    up_first = jnp.where(first, up, 0)
+    goes_p = (d > 0) & ((d < 4) | ((d == 4) & (a == 4)))
+    k = jnp.where(goes_p, d, (RING_Z - d) % RING_Z)
+    same = src[:, None] == src[None, :]
+    order = beams - 1 - q
+
+    def ahead(far):
+        key = far * beams + order
+        hit = same & (far > 0)[None, :] & (key[None, :] > key[:, None])
+        return pick(hit, up_first[None, :], 1)
+
+    pos_p, pos_m = ahead(a), ahead(b)
+    devices = jnp.arange(RING_Y * RING_Z, dtype=jnp.int32)
+    from_dev = devices[:, None] == src[None, :]
+    starts, counts, total = [], [], jnp.int32(0)
+    for far, step in ((a, 1), (b, -1)):
+        count = [
+            pick(from_dev & (far >= j)[None, :], up_first[None, :], 1).reshape(RING_Y, RING_Z)
+            for j in range(1, 5)
+        ]
+        held = [jnp.roll(count[j], step * j, axis=1) for j in range(4)]
+        start = [jnp.zeros((RING_Y, RING_Z), jnp.int32)]
+        for j in range(1, 4):
+            start.append(
+                jnp.maximum(
+                    start[-1] + held[j - 1], jnp.roll(start[-1], step, axis=1) + WAIT
+                )
+            )
+        for j in range(4):
+            total = jnp.maximum(total, jnp.max(jnp.where(held[j] > 0, start[j] + held[j], 0)))
+        starts.append(jnp.stack(start).reshape(4, -1))
+        counts.append(jnp.stack(held).reshape(4, -1))
+    start_all = jnp.concatenate(starts).reshape(-1)
+    node = sy * RING_Z + jnp.where(goes_p, dz + RING_Z - 1, dz + 1) % RING_Z
+    cell = (jnp.where(goes_p, 0, 4) + k - 1) * (RING_Y * RING_Z) + node
+    cells = jnp.arange(start_all.shape[0], dtype=jnp.int32)
+    arrive = pick(cell[:, None] == cells[None, :], start_all[None, :], 1)
+    arrive = jnp.where(d == 0, -WAIT, arrive + jnp.where(goes_p, pos_p, pos_m))
+    turn = (dy - sy) % RING_Y
+    ready = (arrive + WAIT) // 2
+    lane = jnp.where(turn > 0, (sy * RING_Z + dz) * RING_Y + turn, -1 - every)
+    rank_key = ready * beams + every
+    same_lane = lane[:, None] == lane[None, :]
+    before = same_lane & (rank_key[None, :] < rank_key[:, None])
+    queued = pick(before, up[None, :], 1)
+    upto = same_lane & (rank_key[None, :] <= rank_key[:, None])
+    slot = queued + jnp.max(jnp.where(upto, (ready - queued)[None, :], -(2**20)), axis=1)
+    y_total = jnp.max(jnp.where(turn > 0, slot + up, 0))
+    fits = (total <= Z_SLOTS) & (y_total <= Y_SLOTS)
+
+    mine = rank * local + jnp.arange(local, dtype=jnp.int32)
+    page_ids = jnp.arange(pages, dtype=jnp.int32)
+    own_page = pick(
+        (q[:, None] == mine[None, :])[:, :, None], page_table[None, :, :], 1
+    )
+    is_own = src == rank
+    live = page_ids[None, :] < up[:, None]
+    t = jnp.arange(Z_SLOTS, dtype=jnp.int32)
+    tables = []
+    row, col = rank // RING_Z, rank % RING_Z
+    for side, (far, pos, step) in enumerate(((a, pos_p, 1), (b, pos_m, -1))):
+        sends = (is_own & first & (far > 0))[:, None] & live
+        at = jnp.where(sends, pos[:, None] + page_ids[None, :], -1)
+        table = pick(
+            at.reshape(-1)[:, None] == t[None, :], own_page.reshape(-1)[:, None], 0
+        )
+        behind = row * RING_Z + (col - step) % RING_Z
+        for j in range(1, 4):
+            lo = lax.dynamic_index_in_dim(starts[side][j], rank, keepdims=False)
+            n = lax.dynamic_index_in_dim(counts[side][j], rank, keepdims=False)
+            was = lax.dynamic_index_in_dim(starts[side][j - 1], behind, keepdims=False)
+            inside = (t >= lo) & (t < lo + n)
+            table = jnp.where(inside, pool + side * Z_SLOTS + t - lo + was, table)
+        tables.append(table)
+    base = jnp.where(goes_p, pool, pool + Z_SLOTS) + arrive
+    held_at = jnp.where(
+        (d == 0)[:, None], own_page, base[:, None] + page_ids[None, :]
+    )
+    s = jnp.arange(Y_SLOTS, dtype=jnp.int32)
+    for way in (1, 3, 2):
+        sends = ((turn == way) & (sy == row) & (dz == col))[:, None] & live
+        at = jnp.where(sends, slot[:, None] + page_ids[None, :], -1)
+        tables.append(
+            pick(at.reshape(-1)[:, None] == s[None, :], held_at.reshape(-1)[:, None], 0)
+        )
+
+    def own(x):
+        return lax.dynamic_slice_in_dim(x, rank * local, local)
+
+    live_m, turn_m = own(live), own(turn)
+    lands = jnp.where(turn_m == 1, 0, jnp.where(turn_m == 3, Y_SLOTS, 2 * Y_SLOTS)) + own(slot)
+    in_store = (turn_m == 0)[:, None] & live_m
+    in_land = (turn_m > 0)[:, None] & live_m
+    tables.append(jnp.where(in_store, own(held_at), 0).reshape(-1))
+    tables.append(jnp.where(in_land, lands[:, None] + page_ids[None, :], 0).reshape(-1))
+    tables.append(in_land.astype(jnp.int32).reshape(-1))
+    tables.extend(fresh_at)
+    child_len = own(pick(q[:, None] == every[None, :], lengths[None, :], 1))
+    return fits, jnp.concatenate(tables), child_len, own(q)
+
+
+def fresh_rows(page_table, own_len):
+    local, pages = page_table.shape
+    slots = jnp.arange(local * pages, dtype=jnp.int32)
+    page_ids = jnp.arange(pages, dtype=jnp.int32)
+    last = pick(page_ids[None, :] == (own_len // 128)[:, None], page_table, 1)
+    hit = last[:, None] == slots[None, :]
+    at = pick(hit, (own_len % 128 + 1)[:, None], 0) - 1
+    return at, pick(hit, jnp.arange(local, dtype=jnp.int32)[:, None], 0)
+
+
+def moving(tab, fk, fv, kp, vp, nk, nv, store, land_z, land_y, relay, buf_z, buf_y, *sems):
+    send_z, recv_z, send_y, recv_y, recv_r, send_r = sems
+    pool = kp.shape[0]
+    me = lax.axis_index("beam")
+    row, col = me // RING_Z, me % RING_Z
+    z_next = row * RING_Z + lax.rem(col + 1, RING_Z)
+    z_last = row * RING_Z + lax.rem(col + RING_Z - 1, RING_Z)
+    y_next = lax.rem(row + 1, RING_Y) * RING_Z + col
+    y_last = lax.rem(row + RING_Y - 1, RING_Y) * RING_Z + col
+    z_to, y_to = (z_next, z_last), (y_next, y_last)
+    mesh_id = pl.DeviceIdType.MESH
+
+    barrier = pltpu.get_barrier_semaphore()
+    for peer in (z_next, z_last, y_next, y_last):
+        pl.semaphore_signal(barrier, inc=1, device_id={"beam": peer}, device_id_type=mesh_id)
+
+    y_tab = 2 * Z_SLOTS
+    out_tab = y_tab + 3 * Y_SLOTS
+    at_tab = out_tab + 3 * pool
+    rows = lax.broadcasted_iota(jnp.int32, (128, 128), 0)
+
+    def fill(i, carry):
+        at, who = tab[at_tab + i], tab[at_tab + pool + i]
+        hit = rows == at
+        for half, (new, old) in enumerate(((fk, kp), (fv, vp))):
+            line = jnp.broadcast_to(new[who], (128, 128))
+            page = jnp.where(hit, line, old[i].astype(jnp.float32))
+            store[i, half * 128 : half * 128 + 128] = page.astype(jnp.bfloat16)
+        return carry
+
+    lax.fori_loop(0, pool, fill, 0)
+    pl.semaphore_wait(barrier, 4)
+
+    def z_copy(side, t, b):
+        return pltpu.make_async_remote_copy(
+            buf_z.at[side * Z_BUFS + b], land_z.at[side * Z_SLOTS + t],
+            send_z.at[side * Z_BUFS + b], recv_z.at[side * Z_SLOTS + t],
+            device_id={"beam": z_to[side]}, device_id_type=mesh_id,
+        )
+
+    def a_copy(side, s, b):
+        return pltpu.make_async_remote_copy(
+            buf_y.at[side * Y_BUFS + b], land_y.at[side * Y_SLOTS + s],
+            send_y.at[side * Y_BUFS + b], recv_y.at[side * Y_SLOTS + s],
+            device_id={"beam": y_to[side]}, device_id_type=mesh_id,
+        )
+
+    def d_copy(side, s, b):
+        return pltpu.make_async_remote_copy(
+            buf_y.at[2 * Y_BUFS + b], relay.at[s],
+            send_y.at[2 * Y_BUFS + b], recv_r.at[s],
+            device_id={"beam": y_to[side]}, device_id_type=mesh_id,
+        )
+
+    def r_copy(side, s):
+        return pltpu.make_async_remote_copy(
+            relay.at[s], land_y.at[2 * Y_SLOTS + s],
+            send_r.at[s], recv_y.at[2 * Y_SLOTS + s],
+            device_id={"beam": y_to[side]}, device_id_type=mesh_id,
+        )
+
+    def z_slot(g, j):
+        t = 4 * g + j
+
+        @pl.when((t >= WAIT) & (t < Z_SLOTS + WAIT))
+        def _():
+            for side in range(2):
+                z_copy(side, t - WAIT, 0).wait_recv()
+                at = side * Z_SLOTS + t - WAIT
+                store[pool + at] = land_z[at]
+
+        @pl.when(t < Z_SLOTS)
+        def _():
+            b = lax.rem(g, 2) * 4 + j
+            for side in range(2):
+                @pl.when(g >= 2)
+                def _(side=side):
+                    z_copy(side, t - Z_BUFS, b).wait_send()
+
+                buf_z[side * Z_BUFS + b] = store[tab[side * Z_SLOTS + t]]
+                z_copy(side, t, b).start()
+
+    def y_slot(g, j):
+        s = 2 * g + j
+
+        @pl.when(s < Y_SLOTS)
+        def _():
+            b = lax.rem(g, 2) * 2 + j
+
+            @pl.when(g >= 2)
+            def _():
+                a_copy(0, s - Y_BUFS, b).wait_send()
+                a_copy(1, s - Y_BUFS, b).wait_send()
+                d_copy(j, s - Y_BUFS, b).wait_send()
+
+            for way in range(3):
+                buf_y[way * Y_BUFS + b] = store[tab[y_tab + way * Y_SLOTS + s]]
+            d_copy(j, s, b).start()
+            a_copy(0, s, b).start()
+            a_copy(1, s, b).start()
+
+        @pl.when((s >= Y_WAIT) & (s < Y_SLOTS + Y_WAIT))
+        def _():
+            side = 1 - j if Y_WAIT % 2 else j
+            d_copy(side, s - Y_WAIT, 0).wait_recv()
+            r_copy(side, s - Y_WAIT).start()
+
+    def group(g, carry):
+        z_slot(g, 0)
+        z_slot(g, 1)
+        y_slot(g, 0)
+        z_slot(g, 2)
+        z_slot(g, 3)
+        y_slot(g, 1)
+        return carry
+
+    groups = max(-(-(Z_SLOTS + WAIT) // 4), -(-(Y_SLOTS + Y_WAIT) // 2))
+    lax.fori_loop(0, groups, group, 0)
+
+    def drain(i, carry):
+        for j in range(2):
+            s = 2 * i + j
+            a_copy(0, s, 0).wait_recv()
+            a_copy(1, s, 0).wait_recv()
+            r_copy(j, s).wait_recv()
+            r_copy(j, s).wait_send()
+        return carry
+
+    lax.fori_loop(0, Y_SLOTS // 2, drain, 0)
+    for b in range(Z_BUFS):
+        for side in range(2):
+            z_copy(side, 0, b).wait_send()
+    for b in range(Y_BUFS):
+        a_copy(0, 0, b).wait_send()
+        a_copy(1, 0, b).wait_send()
+        d_copy(b % 2, 0, b).wait_send()
+
+    def finish(i, carry):
+        moved = jnp.broadcast_to(tab[out_tab + 2 * pool + i], (128, 128)) > 0
+        for half, out in enumerate((nk, nv)):
+            part = pl.ds(half * 128, 128)
+            here = store[tab[out_tab + i], part].astype(jnp.float32)
+            there = land_y[tab[out_tab + pool + i], part].astype(jnp.float32)
+            out[i] = jnp.where(moved, there, here).astype(jnp.bfloat16)
+        return carry
+
+    lax.fori_loop(0, pool, finish, 0)
+
+
+def move(tables, fresh_k, fresh_v, keys, values):
+    pool = keys.shape[0]
+    page = (256, 128)
+    out = jax.ShapeDtypeStruct(keys.shape, keys.dtype)
+    vmem = pl.BlockSpec(memory_space=pltpu.VMEM)
+    dma = pltpu.SemaphoreType.DMA
+    return pl.pallas_call(
+        moving,
+        out_shape=(out, out),
+        in_specs=[pl.BlockSpec(memory_space=pltpu.SMEM)] + [vmem] * 4,
+        out_specs=(vmem, vmem),
+        scratch_shapes=[
+            pltpu.VMEM((pool + 2 * Z_SLOTS, *page), jnp.bfloat16),
+            pltpu.VMEM((2 * Z_SLOTS, *page), jnp.bfloat16),
+            pltpu.VMEM((3 * Y_SLOTS, *page), jnp.bfloat16),
+            pltpu.VMEM((Y_SLOTS, *page), jnp.bfloat16),
+            pltpu.VMEM((2 * Z_BUFS, *page), jnp.bfloat16),
+            pltpu.VMEM((3 * Y_BUFS, *page), jnp.bfloat16),
+            dma((2 * Z_BUFS,)),
+            dma((2 * Z_SLOTS,)),
+            dma((3 * Y_BUFS,)),
+            dma((3 * Y_SLOTS,)),
+            dma((Y_SLOTS,)),
+            dma((Y_SLOTS,)),
+        ],
+        compiler_params=pltpu.CompilerParams(
+            collective_id=0, has_side_effects=True, vmem_limit_bytes=60 * 1024 * 1024
+        ),
+        name="move_pages",
+    )(tables, fresh_k, fresh_v, keys, values)
 
 
 def sent_to_all(array, axis):
@@ -56,45 +382,9 @@
     heads_local = queries.shape[1] // head_dim
     group = heads_local // kv_local
     beams = lengths.shape[0]
-    capacity = (local_beams + ranks - 1) // ranks
-    slot_cap = capacity * pages
-    buffer_rows = ranks * slot_cap
     everyone = jnp.arange(beams, dtype=jnp.int32)
     page_ids = jnp.arange(pages, dtype=jnp.int32)
     token_grid = page_ids[:, None] * page_length + jnp.arange(page_length, dtype=jnp.int32)[None, :]
-    parent_hit = parents[:, None] == everyone[None, :]
-    parent_len = jnp.sum(jnp.where(parent_hit, lengths[None, :], 0), axis=1)
-    used_pages = parent_len // page_length + 1
-    source = parents // local_beams
-    destination = homes // local_beams
-    earlier = everyone[None, :] < everyone[:, None]
-    same_pair = (
-        (source[:, None] == source[None, :])
-        & (destination[:, None] == destination[None, :])
-        & earlier
-    )
-    offset_table = jnp.sum(jnp.where(same_pair, used_pages[None, :], 0), axis=1)
-    sending = (source == rank)[:, None] & (page_ids[None, :] < used_pages[:, None])
-    dest_rows = destination[:, None] * slot_cap + offset_table[:, None] + page_ids[None, :]
-    dest_rows = jnp.where(sending, dest_rows, buffer_rows)
-    local_parent = jnp.clip(parents - rank * local_beams, 0, local_beams - 1)
-    source_slots = page_table[local_parent]
-    send_table = (
-        jnp.zeros((buffer_rows,), jnp.int32)
-        .at[dest_rows.reshape(-1)]
-        .set(source_slots.reshape(-1), mode="drop")
-    )
-    positions = rank * local_beams + jnp.arange(local_beams, dtype=jnp.int32)
-    child_hit = homes[None, :] == positions[:, None]
-    child_source = jnp.sum(jnp.where(child_hit, source[None, :], 0), axis=1)
-    child_offset = jnp.sum(jnp.where(child_hit, offset_table[None, :], 0), axis=1)
-    child_len = jnp.sum(jnp.where(child_hit, parent_len[None, :], 0), axis=1)
-    child_parent = jnp.sum(jnp.where(child_hit, parents[None, :], 0), axis=1)
-    recv_rows = jnp.clip(
-        child_source[:, None] * slot_cap + child_offset[:, None] + page_ids[None, :],
-        0,
-        buffer_rows - 1,
-    )
     own_len = lax.dynamic_slice_in_dim(lengths, rank * local_beams, local_beams)
     last_page = jnp.take_along_axis(page_table, (own_len // page_length)[:, None], axis=1)[:, 0]
     offset_in = own_len % page_length
@@ -125,23 +415,75 @@
     step_score = jax.nn.sigmoid(total_dot * lax.rsqrt(total_square / width + 1e-06))
     updated = jnp.where(boundary == 1, jnp.minimum(running_min, step_score), running_min)
     every_updated = collect(updated, "beam", 0)
+
+    def slow():
+        capacity = (local_beams + ranks - 1) // ranks
+        slot_cap = capacity * pages
+        buffer_rows = ranks * slot_cap
+        parent_hit = parents[:, None] == everyone[None, :]
+        parent_len = jnp.sum(jnp.where(parent_hit, lengths[None, :], 0), axis=1)
+        used_pages = parent_len // page_length + 1
+        source = parents // local_beams
+        destination = homes // local_beams
+        earlier = everyone[None, :] < everyone[:, None]
+        same_pair = (
+            (source[:, None] == source[None, :])
+            & (destination[:, None] == destination[None, :])
+            & earlier
+        )
+        offset_table = jnp.sum(jnp.where(same_pair, used_pages[None, :], 0), axis=1)
+        sending = (source == rank)[:, None] & (page_ids[None, :] < used_pages[:, None])
+        dest_rows = destination[:, None] * slot_cap + offset_table[:, None] + page_ids[None, :]
+        dest_rows = jnp.where(sending, dest_rows, buffer_rows)
+        local_parent = jnp.clip(parents - rank * local_beams, 0, local_beams - 1)
+        source_slots = page_table[local_parent]
+        send_table = (
+            jnp.zeros((buffer_rows,), jnp.int32)
+            .at[dest_rows.reshape(-1)]
+            .set(source_slots.reshape(-1), mode="drop")
+        )
+        positions = rank * local_beams + jnp.arange(local_beams, dtype=jnp.int32)
+        child_hit = homes[None, :] == positions[:, None]
+        child_source = jnp.sum(jnp.where(child_hit, source[None, :], 0), axis=1)
+        child_offset = jnp.sum(jnp.where(child_hit, offset_table[None, :], 0), axis=1)
+        child_len = jnp.sum(jnp.where(child_hit, parent_len[None, :], 0), axis=1)
+        child_parent = jnp.sum(jnp.where(child_hit, parents[None, :], 0), axis=1)
+        recv_rows = jnp.clip(
+            child_source[:, None] * slot_cap + child_offset[:, None] + page_ids[None, :],
+            0,
+            buffer_rows - 1,
+        )
+        moved_keys, moved_values = (
+            lax.all_to_all(keys_now[send_table], "beam", split_axis=0, concat_axis=0, tiled=True),
+            lax.all_to_all(values_now[send_table], "beam", split_axis=0, concat_axis=0, tiled=True),
+        )
+        shape = (local_beams * pages, page_length, head_dim)
+        return moved_keys[recv_rows].reshape(shape), moved_values[recv_rows].reshape(shape)
+
+    fits, tables, child_len, child_parent = plan(
+        parents, homes, lengths, page_table, fresh_rows(page_table, own_len), rank
+    )
+
+    def fast():
+        shape = (local_beams * pages, page_length, head_dim)
+        return move(
+            tables,
+            fresh_keys.astype(jnp.float32)[:, None, :],
+            fresh_values.astype(jnp.float32)[:, None, :],
+            key_pool.reshape(shape),
+            value_pool.reshape(shape),
+        )
+
     child_score = jnp.sum(
         jnp.where(child_parent[:, None] == everyone[None, :], every_updated[None, :], 0.0), axis=1
     )
-    moved_keys, moved_values = (
-        lax.all_to_all(keys_now[send_table], "beam", split_axis=0, concat_axis=0, tiled=True),
-        lax.all_to_all(values_now[send_table], "beam", split_axis=0, concat_axis=0, tiled=True),
-    )
-    landed_keys = moved_keys[recv_rows]
-    landed_values = moved_values[recv_rows]
-    live_child = (token_grid[None] <= child_len[:, None, None])[:, :, None, :, None]
+    landed_keys, landed_values = lax.cond(fits, fast, slow)
+    live_child = (token_grid[None] <= child_len[:, None, None]).reshape(
+        local_beams * pages, 1, page_length, 1
+    )
     zero = jnp.zeros((), landed_keys.dtype)
-    new_keys = jnp.where(live_child, landed_keys, zero).reshape(
-        local_beams * pages, kv_local, page_length, head_dim
-    )
-    new_values = jnp.where(live_child, landed_values, zero).reshape(
-        local_beams * pages, kv_local, page_length, head_dim
-    )
+    new_keys = jnp.where(live_child, landed_keys[:, None], zero)
+    new_values = jnp.where(live_child, landed_values[:, None], zero)
     return (attention, step_score, child_score, new_keys, new_values)
 
 

time: 271 us -> 236 us (0.87); the launches traced: 266 us -> 235 us
  waiting for transfers between devices: 180 us -> 7.36 us
  Pallas kernels: 0 us -> 143 us
  starting transfers between devices: 31.8 us -> 13.2 us
  other arithmetic: 8.64 us -> 25.3 us
  between operations: 0.95 us -> 14.4 us
  local copies, waits for them, and re-layouts: 41.7 us -> 28.3 us
    all_to_all x2 -> x0, waiting for transfers between devices: 176 us -> none  [the longest x1 89.5 us: per_device(): lax.all_to_all(keys_now[send_table], 'beam', split_axis=0, concat_axis=0,...]
    pallas_call x0 -> x1, Pallas kernels: none -> 143 us  [move(): pl.pallas_call(moving, out_shape=(out, out), in_specs=[pl.BlockSpec(memor...]
    gather x5 -> x0, local copies, waits for them, and re-layouts: 16.2 us -> none  [the longest x1 4.65 us: per_device(): keys_now[send_table]]
    all_to_all x2 -> x0, starting transfers between devices: 14.8 us -> none  [the longest x1 9.41 us: per_device(): lax.all_to_all(values_now[send_table], 'beam', split_axis=0, concat_axis=...]
    select_n x8 -> x7, other arithmetic: 0.46 us -> 11.1 us  [the longest x2 6.19 us: plan(): table = jnp.where(inside, pool + side * Z_SLOTS + t - lo + was, table)]
    scatter x1 -> x0, local copies, waits for them, and re-layouts: 8.04 us -> none  [per_device(): send_table = jnp.zeros((buffer_rows,), jnp.int32).at[dest_rows.reshape(-1...]
    dynamic_slice x0 -> x13, local copies, waits for them, and re-layouts: none -> 6.54 us  [the longest x6 3.73 us: plan(): n = lax.dynamic_index_in_dim(counts[side][j], rank, keepdims=False)]
    reduce_max x0 -> x7, other arithmetic: none -> 5.38 us  [the longest x4 2.7 us: plan(): jnp.max(jnp.where(held[j] > 0, start[j] + held[j], 0))]
  transfers between devices with their start and end apart: 4 -> 2, of which waited for: 3 -> 2; matrix products, arithmetic and copies ran while one was open for 9% -> 2% of each run, Pallas kernels for 0% -> 0%
where the time goes in v1:
time: 236 us; the launch traced here: 235 us
  Pallas kernels  143 us (61%)
  local copies, waits for them, and re-layouts  28.3 us (12%)
  other arithmetic  25.3 us (11%)
  between operations  14.4 us (6%)
  starting transfers between devices  13.2 us (6%)
  waiting for transfers between devices  7.36 us (3%)
  matrix products  3 us (1%)
    pallas_call x1, Pallas kernels, move(): pl.pallas_call(moving, out_shape=(out, out), in_specs=[pl.BlockSpec(memor...  143 us
    all_to_all x2, starting transfers between devices, sent_to_all(): return lax.all_to_all(copies, axis, split_axis=0, concat_axis=0, tiled=True)  13.2 us
    all_to_all x2, waiting for transfers between devices, sent_to_all(): return lax.all_to_all(copies, axis, split_axis=0, concat_axis=0, tiled=True)  7.36 us
    select_n x2, other arithmetic, plan(): table = jnp.where(inside, pool + side * Z_SLOTS + t - lo + was, table)  6.19 us
    select_n x1, other arithmetic, per_device(): new_values = jnp.where(live_child, landed_values[:, None], zero)  4.79 us
  transfers between devices with their start and end apart: 2, of which 2 were waited for; matrix products, arithmetic and copies ran while one was open for 2% of the time, Pallas kernels for 0%

profile of v1, /device:TPU:1, one launch (start us, length us, event | category | flops | bytes accessed | tf_op | source)
XLA Modules:
  0.0 234.8 jit_solution(8418623632610708279)
XLA Ops:
  0.7 0.9 select_reduce_fusion.11
  1.6 1.7 select_reduce_fusion.7
  10.0 0.8 select_reduce_fusion.4
  12.4 0.8 broadcast_add_fusion.1
  17.6 0.7 fusion.69
  20.8 0.7 fusion.65
  30.2 1.3 copy.104
  31.5 1.0 copy-done.2
  40.6 3.1 %and_select_fusion.2 = s32[80]{0:T(128)S(1)} fusion(s32[80]{0:T(128)S(1)} %get-tuple-element.149, s32[]{:T(128)S(6)} %add.1266, s32[]{:T(128)} %bitcast.50, s32[]{:T(128)} %bitcast.49, s32[]{:T(128)S(6)} %add.1263, s32[]{:T(128)} %bitcast.47, s32[]{:T(128)} %bitcast.46, s32[]{:T(128)S(6)} %add.1256, s32[]{:T(128)} %bitcast.44), kind=kLoop, calls=%fused_computation.254 | loop fusion | flops 1440 | bytes 672 | tf_op jit(solution)/shard_map/jit(_where)/select_n | solution.py:115
  43.7 3.1 %and_select_fusion.5 = s32[80]{0:T(128)S(1)} fusion(s32[80]{0:T(128)S(1)} %get-tuple-element.150, s32[]{:T(128)S(6)} %add.1251, s32[]{:T(128)} %bitcast.42, s32[]{:T(128)} %bitcast.41, s32[]{:T(128)S(6)} %add.1248, s32[]{:T(128)} %bitcast.39, s32[]{:T(128)} %bitcast.38, s32[]{:T(128)S(6)} %add.1240, s32[]{:T(128)} %bitcast.36), kind=kLoop, calls=%fused_computation.258 | loop fusion | flops 1440 | bytes 672 | tf_op jit(solution)/shard_map/jit(_where)/select_n | solution.py:115
  46.9 2.3 scatter_fusion
  49.2 1.3 scatter_fusion.1
  50.9 3.8 %gather_fusion.5 = bf16[64,128,128]{2,1,0:T(8,128)(2,1)} fusion(bf16[64,128,128]{2,1,0:T(8,128)(2,1)} %scatter_fusion, s32[1024]{0:T(1024)S(1)} %pad_clamp_fusion.3), kind=kCustom, calls=%fused_computation.5 | custom fusion | bytes 4194560 | tf_op jit(solution)/shard_map/gather | solution.py:398
  54.7 2.1 gather_fusion.6
  56.8 2.5 %fusion.86 = (f32[16,8]{1,0:T(8,128)S(1)}, f32[16,8,4,128]{3,1,2,0:T(8,128)S(1)}) fusion(bf16[16,4,128,128]{3,2,1,0:T(8,128)(2,1)} %bitcast.118, bf16[16,8,128,1]{2,1,0,3:T(8,128)(2,1)S(1)} %bitcast.120, pred[16,4,128]{2,1,0:T(4,128)(4,1)S(1)} %broadcast_compare_fusion.3), kind=kOutput, calls=%fused_computation.347 | convolution fusion | flops 16973696 | bytes 2400768 | tf_op jit(solution)/shard_map/bhgd,bphtd->bhgpt/dot_general | solution.py:402
  60.2 144.4 %conditional.1 = ((bf16[64,128,128]{2,1,0:T(8,128)(2,1)}, bf16[64,128,128]{2,1,0:T(8,128)(2,1)S(1)})) conditional(s32[]{:T(128)} %convert_element_type.31, (s32[512]{0:T(512)S(1)}, s32[]{:T(128)}, s32[4]{0:T(128)S(1)}, s32[4]{0:T(128)S(1)}, s32[512]{0:T(512)S(1)}, /*index=5*/s32[512]{0:T(512)S(1)}, s32[512]{0:T(512)S(1)}, s32[512]{0:T(512)S(1)}, ...), branch_computations={%region_45.51_spmd, %region_51.52_spmd} | conditional | flops 2707153 | bytes 58868416 | solution.py:480
  61.6 142.9 %move_pages.1 = (bf16[64,128,128]{2,1,0:T(8,128)(2,1)}, bf16[64,128,128]{2,1,0:T(8,128)(2,1)S(1)}) custom-call(s32[612]{0:T(1024)S(1)} %get-tuple-element.43.tab, f32[16,1,128]{2,1,0:T(1,128)} %bitcast.123, f32[16,1,128]{2,1,0:T(1,128)} %bitcast.122, bf16[64,128,128]{2,1,0:T(8,128)(2,1)} %bitcast.116, bf16[64,128,128]{2,1,0:T(8,128)(2,1)} %bitcast.114), custom_call_target="tpu_custom_call" | custom-call | tf_op jit(solution)/shard_map/cond/branch_1_fun/move_pages/pallas_call | solution.py:309
  205.2 6.6 %all-to-all-start.2 = ((f32[8,1,32]{2,1,0:T(1,128)}), f32[8,1,32]{2,1,0:T(1,128)S(1)}, u32[]{:S(2)}, u32[]{:S(2)}) async-start(f32[8,1,32]{2,1,0:T(1,128)} %broadcast_in_dim.511), calls=%async_computation.2 | async-start | bytes 8192 | tf_op jit(solution)/shard_map/all_to_all | solution.py:337
  212.2 4.2 %all-to-all-done.2 = f32[8,1,32]{2,1,0:T(1,128)S(1)} async-done(((f32[8,1,32]{2,1,0:T(1,128)}), f32[8,1,32]{2,1,0:T(1,128)S(1)}, u32[]{:S(2)}, u32[]{:S(2)}) %all-to-all-start.2) | async-done | bytes 1056 | tf_op jit(solution)/shard_map/all_to_all | solution.py:337
  217.6 6.5 %all-to-all-start.3 = ((f32[32,1,16]{2,1,0:T(1,128)}), f32[32,1,16]{2,1,0:T(1,128)S(1)}, u32[]{:S(2)}, u32[]{:S(2)}) async-start(f32[32,1,16]{2,1,0:T(1,128)} %broadcast_in_dim.514), calls=%async_computation.3 | async-start | bytes 32768 | tf_op jit(solution)/shard_map/all_to_all | solution.py:337
  224.1 4.8 %select_bitcast_fusion = (bf16[64,1,128,128]{3,2,1,0:T(8,128)(2,1)}, bf16[64,1,128,128]{3,2,1,0:T(8,128)(2,1)}) fusion(bf16[64,128,128]{2,1,0:T(8,128)(2,1)S(1)} %get-tuple-element.56, pred[64,128]{1,0:T(8,128)(4,1)S(1)} %broadcast_compare_fusion.2, bf16[64,128,128]{2,1,0:T(8,128)(2,1)} %get-tuple-element.55), kind=kLoop, calls=%fused_computation.53 | loop fusion | flops 2097152 | bytes 8396800 | tf_op jit(solution)/shard_map/jit(_where)/select_n | solution.py:486
  229.6 3.2 %all-to-all-done.3 = f32[32,1,16]{2,1,0:T(1,128)S(1)} async-done(((f32[32,1,16]{2,1,0:T(1,128)}), f32[32,1,16]{2,1,0:T(1,128)S(1)}, u32[]{:S(2)}, u32[]{:S(2)}) %all-to-all-start.3) | async-done | bytes 2080 | tf_op jit(solution)/shard_map/all_to_all | solution.py:337
  233.3 0.7 reduce.33
  234.1 0.7 select_reduce_fusion.27
  (186 shorter events, 24.4 us)
Async XLA Ops:
  0.6 14.3 %copy-start = (s32[16,4]{0,1:T(4,128)S(1)}, s32[16,4]{0,1:T(4,128)}, u32[]{:S(2)}) copy-start(s32[16,4]{0,1:T(4,128)} %param.19) | copy-start | bytes 772
  13.5 16.7 %copy-start.3 = (bf16[64,1,128,128]{3,2,1,0:T(8,128)(2,1)S(1)}, bf16[64,1,128,128]{3,2,1,0:T(8,128)(2,1)}, u32[]{:S(2)}) copy-start(bf16[64,1,128,128]{3,2,1,0:T(8,128)(2,1)} %param.17) | copy-start | bytes 6291460
  30.2 2.4 %copy-start.2 = (bf16[64,1,128,128]{3,2,1,0:T(8,128)(2,1)S(1)}, bf16[64,1,128,128]{3,2,1,0:T(8,128)(2,1)}, u32[]{:S(2)}) copy-start(bf16[64,1,128,128]{3,2,1,0:T(8,128)(2,1)} %param.18) | copy-start | bytes 6291460
  32.5 14.4 %copy-start.9 = (bf16[16,128]{1,0:T(8,128)(2,1)S(1)}, bf16[16,128]{1,0:T(8,128)(2,1)}, u32[]{:S(2)}) copy-start(bf16[16,128]{1,0:T(8,128)(2,1)} %param.15) | copy-start | bytes 12292
  32.5 16.7 %copy-start.8 = (bf16[16,128]{1,0:T(8,128)(2,1)S(1)}, bf16[16,128]{1,0:T(8,128)(2,1)}, u32[]{:S(2)}) copy-start(bf16[16,128]{1,0:T(8,128)(2,1)} %param.16) | copy-start | bytes 12292
  32.5 18.3 %copy-start.6 = (bf16[16,1024]{1,0:T(8,128)(2,1)S(1)}, bf16[16,1024]{1,0:T(8,128)(2,1)}, u32[]{:S(2)}) copy-start(bf16[16,1024]{1,0:T(8,128)(2,1)} %param.14) | copy-start | bytes 98308
  54.7 2.1 copy-start.11
  56.8 2.7 %copy-start.4 = (bf16[64,128,128]{2,1,0:T(8,128)(2,1)S(1)}, bf16[64,128,128]{2,1,0:T(8,128)(2,1)}, u32[]{:S(2)}) copy-start(bf16[64,128,128]{2,1,0:T(8,128)(2,1)} %gather_fusion.6) | copy-start | bytes 6291460
  56.8 3.3 %copy-start.5 = (s32[512]{0:T(512)S(1)}, s32[512]{0:T(512)}, u32[]{:S(2)}) copy-start(s32[512]{0:T(512)} %param.24) | copy-start | bytes 6148
  56.8 3.3 %copy-start.7 = (s32[512]{0:T(512)S(1)}, s32[512]{0:T(512)}, u32[]{:S(2)}) copy-start(s32[512]{0:T(512)} %param.25) | copy-start | bytes 6148
  56.8 3.3 %copy-start.10 = (s32[512]{0:T(512)S(1)}, s32[512]{0:T(512)}, u32[]{:S(2)}) copy-start(s32[512]{0:T(512)} %param.20) | copy-start | bytes 6148
  60.2 156.2 %copy-start.12 = (f32[16]{0:T(128)S(1)}, f32[16]{0:T(128)}, u32[]{:S(2)}) copy-start(f32[16]{0:T(128)} %param.22) | copy-start | bytes 196
  60.2 156.2 %copy-start.13 = (s32[16]{0:T(128)S(1)}, s32[16]{0:T(128)}, u32[]{:S(2)}) copy-start(s32[16]{0:T(128)} %param.23) | copy-start | bytes 196
  205.2 11.2 %all-to-all-start.2 = ((f32[8,1,32]{2,1,0:T(1,128)}), f32[8,1,32]{2,1,0:T(1,128)S(1)}, u32[]{:S(2)}, u32[]{:S(2)}) async-start(f32[8,1,32]{2,1,0:T(1,128)} %broadcast_in_dim.511), calls=%async_computation.2 | async-start | bytes 8192 | tf_op jit(solution)/shard_map/all_to_all | solution.py:337
  217.6 15.2 %all-to-all-start.3 = ((f32[32,1,16]{2,1,0:T(1,128)}), f32[32,1,16]{2,1,0:T(1,128)S(1)}, u32[]{:S(2)}, u32[]{:S(2)}) async-start(f32[32,1,16]{2,1,0:T(1,128)} %broadcast_in_dim.514), calls=%async_computation.3 | async-start | bytes 32768 | tf_op jit(solution)/shard_map/all_to_all | solution.py:337

commit v2 on v0

--- a/solution.py
+++ b/solution.py
@@ -1,9 +1,522 @@
+import functools
 import math
 
 import jax
 import jax.numpy as jnp
 from jax import lax
+from jax.experimental import pallas as pl
+from jax.experimental.pallas import tpu as pltpu
 from jax.sharding import PartitionSpec as P
+
+WAIT = 4
+Y_WAIT = 3
+Z_BUFS = 8
+Y_BUFS = 4
+RING_Z = 8
+RING_Y = 4
+ROUTES = ((80, 44),)
+PAGE = 128
+LANES = 128
+Z_ROW, Y_ROW, STORE_ROW, LAND_ROW, MOVED_ROW = 0, 2, 5, 6, 7
+FRESH_ROW, WHO_ROW, PARENT_ROW, LENGTH_ROW, OWN_ROW = 8, 9, 10, 11, 12
+MESH = pl.DeviceIdType.MESH
+
+
+def planning(parents_ref, homes_ref, lengths_ref, table_ref, tab_ref, need_ref):
+    f32 = jnp.float32
+    beams = parents_ref.shape[1]
+    local, pages = table_ref.shape
+    pool = local * pages
+    rank = lax.axis_index("beam")
+    rank_f = rank.astype(f32)
+    row_f, col_f = (rank // RING_Z).astype(f32), (rank % RING_Z).astype(f32)
+
+    def iota(shape, dim):
+        return lax.broadcasted_iota(jnp.int32, shape, dim).astype(f32)
+
+    def div(x, n):
+        return jnp.floor(x * (1.0 / n))
+
+    def mod(x, n):
+        return x - n * div(x, n)
+
+    def columns(*rows):
+        packed = jnp.concatenate(
+            list(rows) + [jnp.zeros((8 - len(rows), beams), f32)] * (len(rows) < 8), axis=0
+        )
+        turned = jnp.transpose(packed)
+        return [turned[:, i : i + 1] for i in range(len(rows))]
+
+    def add(mask, column):
+        return jnp.sum(jnp.where(mask, column, 0.0), axis=0, keepdims=True)
+
+    def top(mask, column, least=0.0):
+        return jnp.max(jnp.where(mask, column, least), axis=0, keepdims=True)
+
+    parents, homes, lengths = (
+        ref[...].astype(f32) for ref in (parents_ref, homes_ref, lengths_ref)
+    )
+    parents_c, homes_c, lengths_c = columns(parents, homes, lengths)
+    every = iota((1, beams), 1)
+    every_c = iota((beams, 1), 0)
+    q = add(homes_c == every, parents_c)
+    length = add(every_c == q, lengths_c)
+    up = div(length, PAGE) + 1.0
+    src, dst = div(q, local), div(every, local)
+    sy, sz, dy, dz = div(src, RING_Z), mod(src, RING_Z), div(dst, RING_Z), mod(dst, RING_Z)
+    d = mod(dz - sz + RING_Z, RING_Z)
+    q_c, up_c, d_c = columns(q, up, d)
+    src_c = div(q_c, local)
+    sib = q_c == q
+    far_p = top(sib, jnp.where(d_c < 4, d_c, 0.0))
+    far_m = top(sib, jnp.where(d_c > 4, RING_Z - d_c, 0.0))
+    far_4 = top(sib, jnp.where(d_c == 4, 1.0, 0.0)) > 0
+    first = top(sib & (every_c < every), 1.0) == 0
+    plus4 = far_4 & ((far_p > far_m) | ((far_p == far_m) & (mod(q, 2) == 1)))
+    a = jnp.where(plus4, 4.0, far_p)
+    b = jnp.where(far_4 & jnp.logical_not(plus4), 4.0, far_m)
+    up_first = jnp.where(first, up, 0.0)
+    goes_p = (d > 0) & ((d < 4) | ((d == 4) & (a == 4)))
+    k = jnp.where(goes_p, d, mod(RING_Z - d, RING_Z))
+    a_c, b_c, upf_c = columns(a, b, up_first)
+    same = src_c == src
+    order, order_c = beams - 1 - q, beams - 1 - q_c
+    pos_p = add(
+        same & (a_c * beams + order_c > a * beams + order), jnp.where(a_c > 0, upf_c, 0.0)
+    )
+    pos_m = add(
+        same & (b_c * beams + order_c > b * beams + order), jnp.where(b_c > 0, upf_c, 0.0)
+    )
+
+    weights = jnp.concatenate(
+        [jnp.where(far >= j, up_first, 0.0) for far in (a, b) for j in range(1, 5)], axis=0
+    )
+    lane = iota((1, LANES), 1)
+    count = jnp.dot(weights, jnp.where(src_c == lane, 1.0, 0.0), preferred_element_type=f32)
+    at_z = mod(lane, RING_Z)
+
+    def back(x, n):
+        n = n % RING_Z
+        if n == 0:
+            return x
+        full = jnp.broadcast_to(x, (8, LANES))
+        near = pltpu.roll(full, n, 1)
+        wrap = pltpu.roll(full, LANES + n - RING_Z, 1)
+        return jnp.where(at_z >= n, near, wrap)[:1]
+
+    starts, helds, total = [], [], jnp.zeros((1, LANES), f32)
+    for side in range(2):
+        step = 1 - 2 * side
+        held = [back(count[4 * side + j : 4 * side + j + 1], step * j) for j in range(4)]
+        start = [jnp.zeros((1, LANES), f32)]
+        for j in range(1, 4):
+            start.append(jnp.maximum(start[-1] + held[j - 1], back(start[-1], step) + WAIT))
+        for j in range(4):
+            total = jnp.maximum(total, jnp.where(held[j] > 0, start[j] + held[j], 0.0))
+        starts.append(start)
+        helds.append(held)
+    z_total = jnp.max(total)
+    node = sy * RING_Z + mod(jnp.where(goes_p, dz + RING_Z - 1, dz + 1), RING_Z)
+    spots = jnp.where(iota((LANES, 1), 0) == node, 1.0, 0.0)
+    seen = jnp.dot(
+        jnp.concatenate(starts[0] + starts[1], axis=0), spots,
+        preferred_element_type=f32, precision=lax.Precision.HIGHEST,
+    )
+    seen = jnp.floor(seen + 0.5)
+    cell = jnp.where(goes_p, 0.0, 4.0) + k - 1
+    arrive = jnp.zeros((1, beams), f32)
+    for j in range(8):
+        arrive = jnp.where(cell == j, seen[j : j + 1], arrive)
+    arrive = jnp.where(d == 0, -1.0 * WAIT, arrive + jnp.where(goes_p, pos_p, pos_m))
+    turn = mod(dy - sy + RING_Y, RING_Y)
+    ready = div(arrive + WAIT, 2)
+    queue = jnp.where(turn > 0, (sy * RING_Z + dz) * RING_Y + turn, -1 - every)
+    rank_key = ready * beams + every
+    queue_c, rank_c, ready_c, pos_p_c, pos_m_c, arrive_c, turn_c, goes_c = columns(
+        queue, rank_key, ready, pos_p, pos_m, arrive, turn, jnp.where(goes_p, 1.0, 0.0)
+    )
+    same_queue = queue_c == queue
+    queued = add(same_queue & (rank_c < rank_key), up_c)
+    (queued_c,) = columns(queued)
+    slot = queued + top(same_queue & (rank_c <= rank_key), ready_c - queued_c, -1e6)
+    y_total = jnp.max(jnp.where(turn > 0, slot + up, 0.0))
+    need_ref[0] = z_total.astype(jnp.int32)
+    need_ref[1] = y_total.astype(jnp.int32)
+
+    (slot_c,) = columns(slot)
+    table = table_ref[...].astype(f32)
+    mine = jnp.where(q_c == rank_f * local + iota((1, local), 1), 1.0, 0.0)
+    own_page = jnp.dot(mine, table, preferred_element_type=f32)
+    own_c = [own_page[:, p : p + 1] for p in range(pages)]
+    first_c = upf_c > 0
+    is_own_c = src_c == rank_f
+    tables = []
+    for side, (far_c, pos_c) in enumerate(((a_c, pos_p_c), (b_c, pos_m_c))):
+        step = 1 - 2 * side
+        sends = is_own_c & first_c & (far_c > 0)
+        line = jnp.zeros((1, LANES), f32)
+        for p in range(pages):
+            at = jnp.where(sends & (up_c > p), pos_c + p, -1.0)
+            line += add(at == lane, own_c[p])
+        for j in range(1, 4):
+            pick = lambda x: jnp.sum(jnp.where(lane == rank_f, x, 0.0), axis=1, keepdims=True)
+            lo, n = pick(starts[side][j]), pick(helds[side][j])
+            was = pick(back(starts[side][j - 1], step))
+            line = jnp.where(
+                (lane >= lo) & (lane < lo + n), pool + side + 2 * (lane - lo + was), line
+            )
+        tables.append(line)
+    here_c = d_c == 0
+    base_c = jnp.where(goes_c > 0, pool * 1.0, pool + 1.0) + 2 * arrive_c
+    held_c = [jnp.where(here_c, own_c[p], base_c + 2 * p) for p in range(pages)]
+    sy_c = div(src_c, RING_Z)
+    dz_c = mod(div(every_c, local), RING_Z)
+    at_me = (sy_c == row_f) & (dz_c == col_f)
+    for way in (1.0, 3.0, 2.0):
+        line = jnp.zeros((1, LANES), f32)
+        for p in range(pages):
+            at = jnp.where(at_me & (turn_c == way) & (up_c > p), slot_c + p, -1.0)
+            line += add(at == lane, held_c[p])
+        tables.append(line)
+    way_c = jnp.where(turn_c == 1, 0.0, jnp.where(turn_c == 3, 1.0, 2.0))
+    child = every_c == rank_f * local + div(lane, pages)
+    from_store, from_land, moved = [jnp.zeros((1, LANES), f32)] * 3
+    for p in range(pages):
+        hit = child & (mod(lane, pages) == p) & (lane < pool) & (up_c > p)
+        from_store += add(hit & (turn_c == 0), held_c[p])
+        from_land += add(hit & (turn_c > 0), 3 * (slot_c + p) + way_c)
+        moved += add(hit & (turn_c > 0), 1.0)
+    tables += [from_store, from_land, moved]
+    owner = rank_f * local + iota((local, 1), 0)
+    own_len = jnp.sum(jnp.where(every == owner, lengths, 0.0), axis=1, keepdims=True)
+    fresh, who = jnp.zeros((1, LANES), f32), jnp.zeros((1, LANES), f32)
+    for p in range(pages):
+        hit = (table[:, p : p + 1] == lane) & (div(own_len, PAGE) == p)
+        fresh += add(hit, mod(own_len, PAGE) + 1)
+        who += add(hit, iota((local, 1), 0))
+    length_c = jnp.sum(jnp.where(q_c == every, lengths, 0.0), axis=1, keepdims=True)
+    mine_lane = (every_c == rank_f * local + lane) & (lane < local)
+    tables += [fresh - 1, who, add(mine_lane, q_c), add(mine_lane, length_c)]
+    tables.append(add(mine_lane, lengths_c))
+    tables += [jnp.zeros((1, LANES), f32)] * (16 - len(tables))
+    tab_ref[...] = jnp.concatenate(tables, axis=0).astype(jnp.int32)
+
+
+def plan(parents, homes, lengths, page_table):
+    vmem = pl.BlockSpec(memory_space=pltpu.VMEM)
+    return pl.pallas_call(
+        planning,
+        out_shape=(
+            jax.ShapeDtypeStruct((16, LANES), jnp.int32),
+            jax.ShapeDtypeStruct((2,), jnp.int32),
+        ),
+        in_specs=[vmem] * 4,
+        out_specs=(vmem, pl.BlockSpec(memory_space=pltpu.SMEM)),
+        name="plan_moves",
+    )(parents[None], homes[None], lengths[None], page_table)
+
+
+def moving(z_slots, y_slots, *refs):
+    tab, pages_of, least, ends, fk, fv, q_ref, sw, kp, vp, att, score, nk, nv = refs[:14]
+    store, land_z, land_y, relay, buf_z, buf_y, sums, land_s, land_u = refs[14:23]
+    send_z, recv_z, send_y, recv_y, recv_r, send_r, send_s, recv_s, send_u, recv_u = refs[23:]
+    pool = kp.shape[0]
+    local, heads, head_dim = q_ref.shape
+    pages = pool // local
+    f32 = jnp.float32
+    me, part = lax.axis_index("beam"), lax.axis_index("mp")
+    parts = lax.axis_size("mp")
+    row, col = me // RING_Z, me % RING_Z
+
+    def at_z(n):
+        return row * RING_Z + lax.rem(col + n, RING_Z)
+
+    def at_y(n):
+        return lax.rem(row + n, RING_Y) * RING_Z + col
+
+    z_to, y_to = (at_z(1), at_z(RING_Z - 1)), (at_y(1), at_y(RING_Y - 1))
+    barrier = pltpu.get_barrier_semaphore()
+
+    def greet(where):
+        pl.semaphore_signal(barrier, inc=1, device_id=where, device_id_type=MESH)
+
+    for n in range(1, RING_Z):
+        greet({"beam": at_z(n)})
+    for n in range(1, RING_Y):
+        greet({"beam": at_y(n)})
+    for n in range(1, parts):
+        greet({"mp": lax.rem(part + n, parts)})
+
+    rows = lax.broadcasted_iota(jnp.int32, (PAGE, head_dim), 0)
+
+    def fill(i, carry):
+        hit = rows == tab[FRESH_ROW, i]
+        who = tab[WHO_ROW, i]
+        for half, (new, old) in enumerate(((fk, kp), (fv, vp))):
+            line = jnp.broadcast_to(new[who], (PAGE, head_dim))
+            page = jnp.where(hit, line, old[i].astype(f32))
+            store[i, half * PAGE : half * PAGE + PAGE] = page.astype(jnp.bfloat16)
+        return carry
+
+    lax.fori_loop(0, pool, fill, 0)
+    pl.semaphore_wait(barrier, RING_Z + RING_Y + parts - 3)
+
+    def remote(source, target, sent, got, where):
+        return pltpu.make_async_remote_copy(
+            source, target, sent, got, device_id=where, device_id_type=MESH
+        )
+
+    def z_copy(side, t, b):
+        b = side * Z_BUFS + b
+        return remote(
+            buf_z.at[b], land_z.at[2 * t + side], send_z.at[b], recv_z.at[2 * t + side],
+            {"beam": z_to[side]},
+        )
+
+    def a_copy(side, s, b):
+        b = side * Y_BUFS + b
+        return remote(
+            buf_y.at[b], land_y.at[3 * s + side], send_y.at[b], recv_y.at[3 * s + side],
+            {"beam": y_to[side]},
+        )
+
+    def d_copy(side, s, b):
+        b = 2 * Y_BUFS + b
+        return remote(buf_y.at[b], relay.at[s], send_y.at[b], recv_r.at[s], {"beam": y_to[side]})
+
+    def r_copy(side, s):
+        return remote(
+            relay.at[s], land_y.at[3 * s + 2], send_r.at[s], recv_y.at[3 * s + 2],
+            {"beam": y_to[side]},
+        )
+
+    def s_copy(n, origin):
+        return remote(
+            sums, land_s.at[origin], send_s.at[n], recv_s.at[origin],
+            {"mp": lax.rem(part + n, parts)},
+        )
+
+    def u_copy(n, origin):
+        spot = land_u.at[row, origin]
+        return remote(spot, spot, send_u.at[n], recv_u.at[origin], {"beam": at_z(n)})
+
+    def v_copy(n, origin):
+        spot = land_u.at[origin]
+        return remote(
+            spot, spot, send_u.at[RING_Z + n], recv_u.at[RING_Z + origin], {"beam": at_y(n)}
+        )
+
+    def z_slot(g, j):
+        t = 4 * g + j
+
+        @pl.when((t >= WAIT) & (t < z_slots + WAIT))
+        def _():
+            for side in range(2):
+                z_copy(side, t - WAIT, 0).wait_recv()
+                at = 2 * (t - WAIT) + side
+                store[pool + at] = land_z[at]
+
+        @pl.when(t < z_slots)
+        def _():
+            b = lax.rem(g, 2) * 4 + j
+            for side in range(2):
+
+                @pl.when(g >= 2)
+                def _(side=side):
+                    z_copy(side, t - Z_BUFS, b).wait_send()
+
+                buf_z[side * Z_BUFS + b] = store[tab[Z_ROW + side, t]]
+                z_copy(side, t, b).start()
+
+    def y_slot(g, j):
+        s = 2 * g + j
+
+        @pl.when(s < y_slots)
+        def _():
+            b = lax.rem(g, 2) * 2 + j
+
+            @pl.when(g >= 2)
+            def _():
+                a_copy(0, s - Y_BUFS, b).wait_send()
+                a_copy(1, s - Y_BUFS, b).wait_send()
+                d_copy(j, s - Y_BUFS, b).wait_send()
+
+            for way in range(3):
+                buf_y[way * Y_BUFS + b] = store[tab[Y_ROW + way, s]]
+            d_copy(j, s, b).start()
+            a_copy(0, s, b).start()
+            a_copy(1, s, b).start()
+
+        @pl.when((s >= Y_WAIT) & (s < y_slots + Y_WAIT))
+        def _():
+            side = 1 - j if Y_WAIT % 2 else j
+            d_copy(side, s - Y_WAIT, 0).wait_recv()
+            r_copy(side, s - Y_WAIT).start()
+
+    def attend(i):
+        keys = jnp.concatenate([store[pages_of[i, p], :PAGE] for p in range(pages)], axis=0)
+        logits = lax.dot_general(
+            q_ref[i], keys, (((1,), (1,)), ((), ())), preferred_element_type=f32
+        ) * (1.0 / math.sqrt(head_dim))
+        token = lax.broadcasted_iota(jnp.int32, logits.shape, 1)
+        logits = jnp.where(token <= tab[OWN_ROW, i], logits, -jnp.inf)
+        powers = jnp.exp(logits - jnp.max(logits, axis=1, keepdims=True))
+        weights = (powers / jnp.sum(powers, axis=1, keepdims=True)).astype(jnp.bfloat16)
+        values = jnp.concatenate([store[pages_of[i, p], PAGE:] for p in range(pages)], axis=0)
+        mixed = jnp.dot(weights, values, preferred_element_type=f32).astype(jnp.bfloat16)
+        att[i] = mixed
+        mixed = mixed.astype(f32)
+        for n, other in enumerate((mixed, sw[...].astype(f32))):
+            total = jnp.sum(jnp.sum(mixed * other, axis=1, keepdims=True), axis=0, keepdims=True)
+            sums[n, i] = jnp.broadcast_to(total, (1, LANES))
+
+    lane = lax.broadcasted_iota(jnp.int32, (1, LANES), 1)
+
+    def tell_sums():
+        land_s[part] = sums[...]
+        for n in range(1, parts):
+            s_copy(n, part).start()
+
+    def tell_updated():
+        for n in range(1, parts):
+            s_copy(n, lax.rem(part + parts - n, parts)).wait_recv()
+        both = land_s[0]
+        for n in range(1, parts):
+            both += land_s[n]
+        updated = jnp.zeros((1, LANES), f32)
+        steps = jnp.zeros((1, LANES), f32)
+        for i in range(local):
+            width = heads * head_dim * parts
+            step = jax.nn.sigmoid(both[1, i] * lax.rsqrt(both[0, i] / width + 1e-06))
+            floor = jnp.broadcast_to(least[i], (1, LANES))
+            ended = jnp.broadcast_to(ends[i], (1, LANES)) == 1
+            new = jnp.where(ended, jnp.minimum(floor, step), floor)
+            steps = jnp.where(lane == i, step, steps)
+            updated = jnp.where(lane == i, new, updated)
+        score[0:1, :] = steps
+        land_u[row, col] = updated
+        for n in range(1, RING_Z):
+            u_copy(n, col).start()
+
+    def tell_row():
+        for n in range(1, RING_Z):
+            u_copy(n, lax.rem(col + RING_Z - n, RING_Z)).wait_recv()
+        for n in range(1, RING_Y):
+            v_copy(n, row).start()
+
+    def give_children():
+        for n in range(1, RING_Y):
+            v_copy(n, lax.rem(row + RING_Y - n, RING_Y)).wait_recv()
+        out = jnp.zeros((1, LANES), f32)
+        for i in range(local):
+            q = tab[PARENT_ROW, i]
+            line = land_u[q // (local * RING_Z), (q // local) % RING_Z]
+            value = jnp.sum(jnp.where(lane == q % local, line, 0.0), axis=1, keepdims=True)
+            out = jnp.where(lane == i, jnp.broadcast_to(value, (1, LANES)), out)
+        score[1:2, :] = out
+        for n in range(1, parts):
+            s_copy(n, part).wait_send()
+        for n in range(1, RING_Z):
+            u_copy(n, col).wait_send()
+        for n in range(1, RING_Y):
+            v_copy(n, row).wait_send()
+
+    def group(g, carry):
+        z_slot(g, 0)
+        z_slot(g, 1)
+        y_slot(g, 0)
+
+        @pl.when(g < local)
+        def _():
+            attend(g)
+
+        z_slot(g, 2)
+        z_slot(g, 3)
+        y_slot(g, 1)
+        for n, act in enumerate((tell_sums, tell_updated, tell_row, give_children)):
+            pl.when(g == local + (0, 1, 2, 3)[n])(act)
+        return carry
+
+    groups = max(-(-(z_slots + WAIT) // 4), -(-(y_slots + Y_WAIT) // 2))
+    lax.fori_loop(0, groups, group, 0)
+
+    def drain(i, carry):
+        for j in range(2):
+            s = 2 * i + j
+            a_copy(0, s, 0).wait_recv()
+            a_copy(1, s, 0).wait_recv()
+            r_copy(j, s).wait_recv()
+            r_copy(j, s).wait_send()
+        return carry
+
+    lax.fori_loop(0, y_slots // 2, drain, 0)
+    for b in range(Z_BUFS):
+        for side in range(2):
+            z_copy(side, 0, b).wait_send()
+    for b in range(Y_BUFS):
+        a_copy(0, 0, b).wait_send()
+        a_copy(1, 0, b).wait_send()
+        d_copy(b % 2, 0, b).wait_send()
+
+    def finish(i, carry):
+        moved = jnp.broadcast_to(tab[MOVED_ROW, i], (PAGE, head_dim)) > 0
+        live = rows + lax.rem(i, pages) * PAGE <= tab[LENGTH_ROW, i // pages]
+        for half, out in enumerate((nk, nv)):
+            side = pl.ds(half * PAGE, PAGE)
+            here = store[tab[STORE_ROW, i], side].astype(f32)
+            there = land_y[tab[LAND_ROW, i], side].astype(f32)
+            page = jnp.where(live, jnp.where(moved, there, here), 0.0)
+            out[i] = page.astype(jnp.bfloat16)
+        return carry
+
+    lax.fori_loop(0, pool, finish, 0)
+
+
+def move(z_slots, y_slots, tables, page_table, running_min, boundary, fresh_k, fresh_v, query,
+         score_weight, keys, values):
+    pool = keys.shape[0]
+    page = (2 * PAGE, keys.shape[2])
+    out = jax.ShapeDtypeStruct(keys.shape, keys.dtype)
+    vmem, smem = pl.BlockSpec(memory_space=pltpu.VMEM), pl.BlockSpec(memory_space=pltpu.SMEM)
+    dma = pltpu.SemaphoreType.DMA
+    parts = lax.axis_size("mp")
+    local = query.shape[0]
+    return pl.pallas_call(
+        functools.partial(moving, z_slots, y_slots),
+        out_shape=(
+            jax.ShapeDtypeStruct(query.shape, query.dtype),
+            jax.ShapeDtypeStruct((2, LANES), jnp.float32),
+            out,
+            out,
+        ),
+        in_specs=[smem] * 4 + [vmem] * 6,
+        out_specs=(vmem,) * 4,
+        scratch_shapes=[
+            pltpu.VMEM((pool + 2 * z_slots, *page), jnp.bfloat16),
+            pltpu.VMEM((2 * z_slots, *page), jnp.bfloat16),
+            pltpu.VMEM((3 * y_slots, *page), jnp.bfloat16),
+            pltpu.VMEM((y_slots, *page), jnp.bfloat16),
+            pltpu.VMEM((2 * Z_BUFS, *page), jnp.bfloat16),
+            pltpu.VMEM((3 * Y_BUFS, *page), jnp.bfloat16),
+            pltpu.VMEM((2, local, 1, LANES), jnp.float32),
+            pltpu.VMEM((parts, 2, local, 1, LANES), jnp.float32),
+            pltpu.VMEM((RING_Y, RING_Z, 1, LANES), jnp.float32),
+            dma((2 * Z_BUFS,)),
+            dma((2 * z_slots,)),
+            dma((3 * Y_BUFS,)),
+            dma((3 * y_slots,)),
+            dma((y_slots,)),
+            dma((y_slots,)),
+            dma((parts,)),
+            dma((parts,)),
+            dma((RING_Z + RING_Y,)),
+            dma((RING_Z + RING_Y,)),
+        ],
+        compiler_params=pltpu.CompilerParams(
+            collective_id=0, has_side_effects=True, vmem_limit_bytes=60 * 1024 * 1024
+        ),
+        name="move_pages",
+    )(tables, page_table, running_min, boundary, fresh_k, fresh_v, query, score_weight, keys, values)
 
 
 def sent_to_all(array, axis):
@@ -33,7 +546,7 @@
     return laid_out(sent_to_all(array, axis), dim)
 
 
-def per_device(
+def whole_exchange(
     queries,
     fresh_keys,
     fresh_values,
@@ -145,6 +658,43 @@
     return (attention, step_score, child_score, new_keys, new_values)
 
 
+def per_device(*args):
+    (queries, fresh_keys, fresh_values, key_pool, value_pool, page_table) = args[:6]
+    (lengths, score_weight, running_min, boundary, parents, homes) = args[6:]
+    local = queries.shape[0]
+    pool, kv, page, head_dim = key_pool.shape
+    tables, need = plan(parents, homes, lengths, page_table)
+    route = jnp.int32(len(ROUTES))
+    for n, (z_slots, y_slots) in reversed(tuple(enumerate(ROUTES))):
+        route = jnp.where((need[0] <= z_slots) & (need[1] <= y_slots), n, route)
+
+    def streamed(z_slots, y_slots):
+        attention, score, new_keys, new_values = move(
+            z_slots,
+            y_slots,
+            tables,
+            page_table,
+            running_min,
+            boundary,
+            fresh_keys.astype(jnp.float32)[:, None, :],
+            fresh_values.astype(jnp.float32)[:, None, :],
+            queries.reshape(local, -1, head_dim),
+            score_weight.reshape(-1, head_dim),
+            key_pool.reshape(pool, page, head_dim),
+            value_pool.reshape(pool, page, head_dim),
+        )
+        return (
+            attention.reshape(queries.shape),
+            score[0, :local],
+            score[1, :local],
+            new_keys.reshape(key_pool.shape),
+            new_values.reshape(value_pool.shape),
+        )
+
+    ways = [functools.partial(streamed, *r) for r in ROUTES]
+    return lax.switch(route, ways + [lambda: whole_exchange(*args)])
+
+
 def solution(mesh):
     in_specs = (
         P("beam", "mp"),

time: 271 us -> 173 us (0.64); the launches traced: 266 us -> 173 us
  waiting for transfers between devices: 180 us -> 0 us
  Pallas kernels: 0 us -> 157 us
  starting transfers between devices: 31.8 us -> 0 us
  local copies, waits for them, and re-layouts: 41.7 us -> 13.1 us
  other arithmetic: 8.64 us -> 1.19 us
  matrix products: 3 us -> 0 us
    all_to_all x4 -> x0, waiting for transfers between devices: 180 us -> none  [the longest x1 89.5 us: per_device(): lax.all_to_all(keys_now[send_table], 'beam', split_axis=0, concat_axis=0,...]
    pallas_call x0 -> x2, Pallas kernels: none -> 157 us  [the longest x1 146 us: move(): pl.pallas_call(functools.partial(moving, z_slots, y_slots), out_shape=(ja...]
    all_to_all x4 -> x0, starting transfers between devices: 31.8 us -> none  [the longest x2 17 us: sent_to_all(): return lax.all_to_all(copies, axis, split_axis=0, concat_axis=0, tiled=True)]
    gather x8 -> x0, local copies, waits for them, and re-layouts: 22.9 us -> none  [the longest x1 4.65 us: per_device(): keys_now[send_table]]
    scatter x3 -> x0, local copies, waits for them, and re-layouts: 11.6 us -> none  [the longest x1 8.04 us: per_device(): send_table = jnp.zeros((buffer_rows,), jnp.int32).at[dest_rows.reshape(-1...]
    unnamed x29 -> x33, local copies, waits for them, and re-layouts: 4.56 us -> 9.74 us
    unnamed x1 -> x0, other arithmetic: 4.74 us -> none
    dot_general x2 -> x0, matrix products: 3 us -> none  [the longest x1 2.46 us: per_device(): jnp.einsum('bhgd,bphtd->bhgpt', query, key_rows, preferred_element_type=j...]
  transfers between devices with their start and end apart: 4 -> 0, of which waited for: 3 -> 0; matrix products, arithmetic and copies ran while one was open for 9% -> 0% of each run, Pallas kernels for 0% -> 0%
where the time goes in v2:
time: 173 us
  Pallas kernels  157 us (91%)
  local copies, waits for them, and re-layouts  13.1 us (8%)
  between operations  2.07 us (1%)
    pallas_call x1, Pallas kernels, move(): pl.pallas_call(functools.partial(moving, z_slots, y_slots), out_shape=(ja...  146 us
    pallas_call x1, Pallas kernels, plan(): pl.pallas_call(planning, out_shape=(jax.ShapeDtypeStruct((16, LANES), jnp...  10.1 us
    unnamed x33, local copies, waits for them, and re-layouts  9.74 us

profile of v2, /device:TPU:1, one launch (start us, length us, event | category | flops | bytes accessed | tf_op | source)
XLA Modules:
  0.0 172.9 jit_solution(16960620778909241409)
XLA Ops:
  0.6 3.2 %copy.107 = bf16[64,1,128,128]{3,2,1,0:T(8,128)(2,1)} copy(bf16[64,1,128,128]{3,2,1,0:T(8,128)(2,1)} %param.17) | data formatting | bytes 4194304
  3.8 0.0 copy-start
  3.8 0.0 copy-start.3
  3.8 0.0 copy-start.7
  3.8 0.0 copy-start.8
  3.9 0.0 copy-start.10
  3.9 0.0 copy-start.11
  3.9 0.0 copy-start.12
  3.9 0.6 copy-done.6
  4.5 0.7 copy.75.table_ref
  5.2 0.0 copy-done.9
  5.2 10.1 %plan_moves.1 = (s32[16,128]{1,0:T(8,128)S(1)}, s32[2]{0:T(128)}) custom-call(s32[1,512]{1,0:T(1,128)S(1)} %bitcast.105, s32[1,512]{1,0:T(1,128)S(1)} %bitcast.110, s32[1,512]{1,0:T(1,128)S(1)} %bitcast.112, s32[16,4]{1,0:T(8,128)} %copy.75.table_ref), custom_call_target="tpu_custom_call" | custom-call | tf_op jit(solution)/shard_map/plan_moves/pallas_call | solution.py:207
  15.3 1.3 fusion.29
  17.9 149.7 %conditional.1 = (f32[16]{0:T(128)S(1)}, f32[16]{0:T(128)S(1)}, bf16[64,1,128,128]{3,2,0,1:T(8,128)(2,1)}, bf16[64,1,128,128]{3,2,0,1:T(8,128)(2,1)}, bf16[16,8,128]{2,1,0:T(8,128)(2,1)S(1)}) conditional(s32[]{:T(128)} %bitcast.42, (bf16[16,128]{1,0:T(8,128)(2,1)S(1)}, bf16[16,128]{1,0:T(8,128)(2,1)S(1)}, bf16[16,1024]{1,0:T(8,128)(2,1)S(1)}, ...), branch_computations={%region_0.1_spmd, %region_1.17_spmd} | conditional | flops 39058764 | bytes 80967640 | solution.py:695
  18.0 0.6 copy.86
  18.6 0.6 broadcast_in_dim.185
  19.2 0.6 broadcast_in_dim.186
  19.8 0.7 copy.78.refs_1_
  20.4 146.5 %move_pages.1 = (bf16[16,8,128]{2,1,0:T(8,128)(2,1)S(1)}, f32[2,128]{1,0:T(2,128)}, bf16[64,128,128]{2,1,0:T(8,128)(2,1)}, bf16[64,128,128]{2,1,0:T(8,128)(2,1)}) custom-call(s32[16,128]{1,0:T(8,128)S(1)} %get-tuple-element.44.refs_0_, s32[16,4]{1,0:T(8,128)} %copy.78.refs_1_, f32[16]{0:T(128)S(1)} %get-tuple-element.46.refs_2_, ...), custom_call_target="tpu_custom_call" | custom-call | tf_op jit(solution)/shard_map/cond/branch_0_fun/move_pages/pallas_call | solution.py:484
  166.9 0.8 slice_bitcast_fusion
  167.7 0.6 copy.90
  168.3 3.3 %copy.109 = bf16[64,1,128,128]{3,2,1,0:T(8,128)(2,1)} copy(bf16[64,1,128,128]{3,2,1,0:T(8,128)(2,1)} %bitcast.97) | data formatting | bytes 4194304
  171.6 0.0 copy-done.14
  171.6 1.3 copy.110
  (18 shorter events, 0.0 us)
Async XLA Ops:
  3.8 0.7 copy-start.6
  3.8 1.4 copy-start.4
  3.8 1.4 copy-start.5
  3.8 1.4 copy-start.9
  3.8 14.1 %copy-start = (bf16[64,1,128,128]{3,2,1,0:T(8,128)(2,1)S(1)}, bf16[64,1,128,128]{3,2,1,0:T(8,128)(2,1)}, u32[]{:S(2)}) copy-start(bf16[64,1,128,128]{3,2,1,0:T(8,128)(2,1)} %param.18) | copy-start | bytes 6291460
  3.8 14.1 %copy-start.3 = (bf16[16,1024]{1,0:T(8,128)(2,1)S(1)}, bf16[16,1024]{1,0:T(8,128)(2,1)}, u32[]{:S(2)}) copy-start(bf16[16,1024]{1,0:T(8,128)(2,1)} %param.14) | copy-start | bytes 98308
  3.8 14.1 %copy-start.7 = (bf16[16,128]{1,0:T(8,128)(2,1)S(1)}, bf16[16,128]{1,0:T(8,128)(2,1)}, u32[]{:S(2)}) copy-start(bf16[16,128]{1,0:T(8,128)(2,1)} %param.15) | copy-start | bytes 12292
  3.8 14.1 %copy-start.8 = (bf16[16,128]{1,0:T(8,128)(2,1)S(1)}, bf16[16,128]{1,0:T(8,128)(2,1)}, u32[]{:S(2)}) copy-start(bf16[16,128]{1,0:T(8,128)(2,1)} %param.16) | copy-start | bytes 12292
  3.9 14.1 %copy-start.10 = (bf16[1024]{0:T(1024)(128)(2,1)S(1)}, bf16[1024]{0:T(1024)(128)(2,1)}, u32[]{:S(2)}) copy-start(bf16[1024]{0:T(1024)(128)(2,1)} %param.21) | copy-start | bytes 6148
  3.9 14.1 %copy-start.11 = (f32[16]{0:T(128)S(1)}, f32[16]{0:T(128)}, u32[]{:S(2)}) copy-start(f32[16]{0:T(128)} %param.22) | copy-start | bytes 196
  3.9 14.1 %copy-start.12 = (s32[16]{0:T(128)S(1)}, s32[16]{0:T(128)}, u32[]{:S(2)}) copy-start(s32[16]{0:T(128)} %param.23) | copy-start | bytes 196
  167.7 3.9 %copy-start.13 = (f32[16]{0:T(128)}, f32[16]{0:T(128)S(1)}, u32[]{:S(2)}) copy-start(f32[16]{0:T(128)S(1)} %get-tuple-element.291) | copy-start | bytes 196
  167.7 3.9 %copy-start.14 = (f32[16]{0:T(128)}, f32[16]{0:T(128)S(1)}, u32[]{:S(2)}) copy-start(f32[16]{0:T(128)S(1)} %get-tuple-element.290) | copy-start | bytes 196
  168.3 3.3 %copy-start.2 = (bf16[64,1,128,128]{3,2,0,1:T(8,128)(2,1)S(1)}, bf16[64,1,128,128]{3,2,0,1:T(8,128)(2,1)}, u32[]{:S(2)}) copy-start(bf16[64,1,128,128]{3,2,0,1:T(8,128)(2,1)} %get-tuple-element.249) | copy-start | bytes 6291460
